TPU v7x, 32 devices: a whole 2x2x4 slice. The times are simulated.
32 devices in a mesh: dev: 32 (over z, y, x, core).
Axes of the slice: x: 2, y: 2, z: 4, core: 2. Of those that a mesh axis runs over, the one named last changes fastest.
Arguments:
- pixels: bfloat16 [96, 64, 16], P('dev'), may hold values from -6 to 6
- embed_w: bfloat16 [96, 16, 8192], P('dev'), may hold values from -1.5 to 1.5
- var_embed: bfloat16 [96, 8192], P('dev'), may hold values from -3 to 3
- key_w: bfloat16 [8192, 8192], P('dev'), may hold values from -0.0625 to 0.0625
- query: float32 [8192], replicated, may hold values from -500 to 500
- value_t: bfloat16 [8192, 8192], P('dev'), may hold values from -0.0625 to 0.0625
- out_w: bfloat16 [8192, 8192], P('dev'), may hold values from -0.0625 to 0.0625
Outputs:
- mixed: bfloat16 [64, 8192], P('dev')
All inputs are finite; a program needn't handle non-finite values.
Results may differ from a plain program's by a relative error of at most 0.012.
The roundings to bfloat16 on the way count: a program that leaves them out, or rounds other values in their place, can miss the bound.
Values may be sent and summed in bfloat16 or wider, within the bound.
A program may use at most 64 MiB of HBM per device.

v0:
```python
import jax
import jax.numpy as jnp
from jax import lax
from jax.sharding import PartitionSpec as P

D = 8192
HEADS = 64
HD = 128
V = 91


def body(pixels, embed_w, var_embed, key_w, query, value_t, out_w):
    group_size = lax.axis_size("dev")
    own_embed = jnp.einsum("vtp,vpd->vtd", pixels, embed_w, preferred_element_type=jnp.float32)
    own_embed = (own_embed + var_embed.astype(jnp.float32)[:, None, :]).astype(jnp.bfloat16)
    grouped = lax.all_to_all(own_embed, "dev", split_axis=1, concat_axis=0, tiled=True)
    key_rows = key_w.shape[0]
    keyq_part = jnp.einsum(
        "dhj,hj->dh",
        key_w.astype(jnp.float32).reshape(key_rows, HEADS, HD),
        query.reshape(HEADS, HD),
        precision=lax.Precision.HIGHEST,
    )
    keyq = lax.all_gather(keyq_part, "dev", axis=0, tiled=True)
    logits = jnp.einsum(
        "vtd,dh->vth", grouped.astype(jnp.float32), keyq, precision=lax.Precision.HIGHEST
    ) / jnp.sqrt(jnp.float32(HD))
    slot = lax.broadcasted_iota(jnp.int32, logits.shape, 0)
    logits = jnp.where(slot < V, logits, -1e30)
    row_max = jnp.max(logits, axis=0, keepdims=True)
    weights = jnp.exp(logits - row_max)
    attn = (weights / jnp.sum(weights, axis=0, keepdims=True)).astype(jnp.bfloat16)
    pooled = jnp.einsum("vth,vtd->thd", attn, grouped, preferred_element_type=jnp.float32).astype(
        jnp.bfloat16
    )
    own_tokens = pooled.shape[0]
    if group_size >= HEADS:
        spread = jnp.repeat(pooled, group_size // HEADS, axis=1)[:, :, None, :]
    else:
        spread = pooled.reshape(own_tokens, group_size, HEADS // group_size, D)
    received = lax.all_to_all(spread, "dev", split_axis=1, concat_axis=0, tiled=True)
    all_tokens = received.shape[0]
    head_share = received.shape[2]
    received = received.reshape(all_tokens, head_share, D)
    columns = value_t.shape[0]
    value_heads = jnp.einsum(
        "thd,hcd->thc",
        received,
        value_t.reshape(head_share, columns // head_share, D),
        preferred_element_type=jnp.float32,
    )
    value_heads = value_heads.reshape(all_tokens, columns).astype(jnp.bfloat16)
    summed = lax.psum_scatter(
        jnp.dot(value_heads, out_w, preferred_element_type=jnp.float32),
        "dev",
        scatter_dimension=0,
        tiled=True,
    )
    return summed.astype(jnp.bfloat16)


def solution(mesh):
    placed = (
        P("dev", None, None),
        P("dev", None, None),
        P("dev", None),
        P("dev", None),
        P(),
        P("dev", None),
        P("dev", None),
    )
    return jax.shard_map(
        body, mesh=mesh, in_specs=placed, out_specs=P("dev", None), check_vma=False
    )
```

profile of v0, /device:TPU:0, one launch (start us, length us, event | category | flops | bytes accessed | tf_op | source)
XLA Modules:
  0.0 285.6 jit_solution(11926075932730230169)
XLA Ops:
  6.5 0.0 copy-start
  6.5 0.9 convert_element_type.26
  7.5 0.2 copy-done
  7.7 1.7 fusion.1
  9.4 4.7 %copy.15 = bf16[3,64,8192]{2,0,1:T(4,128)(2,1)} copy(bf16[3,64,8192]{2,1,0:T(8,128)(2,1)S(1)} %fusion.1) | data formatting | bytes 6291456 | tf_op jit(solution)/shard_map/convert_element_type | solution.py:15
  14.1 7.4 %all-to-all-start = ((bf16[3,64,8192]{2,0,1:T(4,128)(2,1)}), bf16[3,64,8192]{2,0,1:T(4,128)(2,1)}, u32[]{:S(2)}, u32[]{:S(2)}) async-start(bf16[3,64,8192]{2,0,1:T(4,128)(2,1)} %copy.15), calls=%async_computation | async-start | bytes 8388608 | tf_op jit(solution)/shard_map/all_to_all | solution.py:16
  21.6 0.0 copy-start.2
  21.6 0.0 all-gather.2.cloned.1.call-start
  21.6 6.4 %copy.25 = bf16[256,8192]{0,1:T(8,128)(2,1)} copy(bf16[256,8192]{1,0:T(8,128)(2,1)} %param.10) | data formatting | bytes 8388608 | tf_op jit(solution)/shard_map/reshape | solution.py:20
  28.0 0.0 copy-done.2
  28.0 3.9 %fusion.32 = f32[64,1,256]{2,1,0:T(1,128)S(1)} fusion(f32[64,128,1]{1,2,0:T(1,128)S(1)} %bitcast.48, bf16[256,64,128]{0,2,1:T(8,128)(2,1)} %bitcast.44), kind=kOutput, calls=%fused_computation.26 | convolution fusion | flops 25165824 | bytes 4292608 | tf_op jit(solution)/shard_map/dhj,hj->dh/dot_general | solution.py:18
  31.9 0.6 copy.47
  32.5 0.0 all-gather.2.cloned.1.call-update
  32.6 93.2 %all-to-all-done = bf16[3,64,8192]{2,0,1:T(4,128)(2,1)} async-done(((bf16[3,64,8192]{2,0,1:T(4,128)(2,1)}), bf16[3,64,8192]{2,0,1:T(4,128)(2,1)}, u32[]{:S(2)}, u32[]{:S(2)}) %all-to-all-start) | async-done | bytes 3145760 | tf_op jit(solution)/shard_map/all_to_all | solution.py:16
  125.8 7.9 %copy.16 = bf16[3,32,2,8192]{3,2,0,1:T(2,128)(2,1)} copy(bf16[3,32,2,8192]{3,0,2,1:T(4,128)(2,1)} %bitcast) | data formatting | bytes 6291456 | tf_op jit(solution)/shard_map/all_to_all | solution.py:16
  133.7 0.0 all-gather.2.cloned.1.call-done
  133.7 9.0 %fusion.15 = f32[96,2,64]{0,2,1:T(8,128)S(1)} fusion(f32[8192,64]{0,1:T(8,128)} %all-gather.2.cloned.1.call-done, bf16[96,2,8192]{2,1,0:T(2,128)(2,1)} %bitcast.42, pred[96]{0:T(512)(128)(4,1)S(1)} %iota_compare_fusion), kind=kOutput, calls=%fused_computation.13 | convolution fusion | flops 1207984128 | bytes 5292128 | tf_op jit(solution)/shard_map/vtd,dh->vth/dot_general | solution.py:25
  142.7 0.2 fusion.31
  142.9 6.0 %convolution_convert_fusion = bf16[2,64,8192]{2,1,0:T(8,128)(2,1)S(1)} fusion(bf16[96,2,8192]{2,1,0:T(2,128)(2,1)} %bitcast.43, f32[2,64]{1,0:T(2,128)S(1)} %fusion.31, f32[96,2,64]{0,2,1:T(8,128)S(1)} %fusion.15), kind=kOutput, calls=%fused_computation.3 | convolution fusion | flops 202412256 | bytes 5292544 | tf_op jit(solution)/shard_map/vth,vtd->thd/dot_general | solution.py:33
  148.9 2.7 reshape.23
  151.6 6.0 %copy.19 = bf16[2,32,2,8192]{3,2,0,1:T(2,128)(2,1)} copy(bf16[2,32,2,8192]{3,2,1,0:T(2,128)(2,1)} %reshape.23) | data formatting | bytes 4194304 | tf_op jit(solution)/shard_map/reshape | solution.py:40
  157.5 4.1 %all-to-all-start.1 = ((bf16[2,32,2,8192]{3,2,0,1:T(2,128)(2,1)}), bf16[2,32,2,8192]{3,2,0,1:T(2,128)(2,1)S(1)}, u32[]{:S(2)}, u32[]{:S(2)}) async-start(bf16[2,32,2,8192]{3,2,0,1:T(2,128)(2,1)} %copy.19), calls=%async_computation.1 | async-start | bytes 4194304 | tf_op jit(solution)/shard_map/all_to_all | solution.py:41
  161.7 48.7 %all-to-all-done.1 = bf16[2,32,2,8192]{3,2,0,1:T(2,128)(2,1)S(1)} async-done(((bf16[2,32,2,8192]{3,2,0,1:T(2,128)(2,1)}), bf16[2,32,2,8192]{3,2,0,1:T(2,128)(2,1)S(1)}, u32[]{:S(2)}, u32[]{:S(2)}) %all-to-all-start.1) | async-done | bytes 2097184 | tf_op jit(solution)/shard_map/all_to_all | solution.py:41
  210.4 0.0 copy-start.1
  210.4 4.1 %fusion.23 = bf16[2,8,8,128]{3,2,1,0:T(8,128)(2,1)S(1)} fusion(bf16[2,128,8192]{2,1,0:T(8,128)(2,1)} %bitcast.46, bf16[64,2,8192]{2,1,0:T(2,128)(2,1)S(1)} %bitcast.45), kind=kOutput, calls=%fused_computation.15 | convolution fusion | flops 268451840 | bytes 6324224 | tf_op jit(solution)/shard_map/thd,hcd->thc/dot_general | solution.py:46
  214.5 0.0 copy-done.1
  214.5 0.8 fusion.26
  215.4 61.8 %all-reduce.2 = bf16[64,8192]{1,0:T(8,128)(2,1)} all-reduce(f32[64,8192]{1,0:T(8,128)S(1)} %fusion.26), channel_id=2, replica_groups=mesh['dev'=32] {'dev'}, use_global_device_ids=true, to_apply=%region_2.3.clone | all-reduce | flops 524288 | bytes 3145728
  277.2 1.6 dynamic-slice_convert_fusion
  (1 shorter events, 0.0 us)
Async XLA Ops:
  6.5 1.2 copy-start
  14.1 111.7 %all-to-all-start = ((bf16[3,64,8192]{2,0,1:T(4,128)(2,1)}), bf16[3,64,8192]{2,0,1:T(4,128)(2,1)}, u32[]{:S(2)}, u32[]{:S(2)}) async-start(bf16[3,64,8192]{2,0,1:T(4,128)(2,1)} %copy.15), calls=%async_computation | async-start | bytes 8388608 | tf_op jit(solution)/shard_map/all_to_all | solution.py:16
  21.6 6.4 %copy-start.2 = (f32[8192]{0:T(1024)S(1)}, f32[8192]{0:T(1024)}, u32[]{:S(2)}) copy-start(f32[8192]{0:T(1024)} %param.11) | copy-start | bytes 98308
  21.6 112.1 %all-gather.2.cloned.1.call-start = ((), (), s32[]{:S(2)}) async-start(), calls=%async_computation.2 | async-start | bytes 2162688 | tf_op jit(solution)/shard_map/all_gather | solution.py:24
  157.5 52.9 %all-to-all-start.1 = ((bf16[2,32,2,8192]{3,2,0,1:T(2,128)(2,1)}), bf16[2,32,2,8192]{3,2,0,1:T(2,128)(2,1)S(1)}, u32[]{:S(2)}, u32[]{:S(2)}) async-start(bf16[2,32,2,8192]{3,2,0,1:T(2,128)(2,1)} %copy.19), calls=%async_computation.1 | async-start | bytes 4194304 | tf_op jit(solution)/shard_map/all_to_all | solution.py:41
  210.4 4.1 %copy-start.1 = (bf16[256,8192]{1,0:T(8,128)(2,1)S(1)}, bf16[256,8192]{1,0:T(8,128)(2,1)}, u32[]{:S(2)}) copy-start(bf16[256,8192]{1,0:T(8,128)(2,1)} %param.13) | copy-start | bytes 12582916
Sparse Core Ops, SparseCore 0:
  32.7 79.4 all-gather.1
where the time goes:
time: 286 us
  waiting for transfers between devices  142 us (50%)
  blocking collectives  61.8 us (22%)
  local copies, waits for them, and re-layouts  30 us (10%)
  matrix products  25.6 us (9%)
  between operations  13.5 us (5%)
  starting transfers between devices  11.6 us (4%)
    all_to_all x1, waiting for transfers between devices, body(): lax.all_to_all(own_embed, 'dev', split_axis=1, concat_axis=0, tiled=True)  93.2 us
    unnamed x1, blocking collectives  61.8 us
    all_to_all x1, waiting for transfers between devices, body(): lax.all_to_all(spread, 'dev', split_axis=1, concat_axis=0, tiled=True)  48.7 us
    dot_general x1, matrix products, body(): jnp.einsum('vtd,dh->vth', grouped.astype(jnp.float32), keyq, precision=la...  8.99 us
    reshape x2, local copies, waits for them, and re-layouts, body(): spread = pooled.reshape(own_tokens, group_size, HEADS // group_size, D)  8.65 us
    all_to_all x1, local copies, waits for them, and re-layouts, body(): lax.all_to_all(own_embed, 'dev', split_axis=1, concat_axis=0, tiled=True)  7.92 us
    all_to_all x1, starting transfers between devices, body(): lax.all_to_all(own_embed, 'dev', split_axis=1, concat_axis=0, tiled=True)  7.44 us
    reshape x1, local copies, waits for them, and re-layouts, body(): key_w.astype(jnp.float32).reshape(key_rows, HEADS, HD)  6.36 us
  transfers between devices with their start and end apart: 3, of which 2 were waited for; matrix products, arithmetic and copies ran while one was open for 7% of the time, Pallas kernels for 0%

commit v1 on v0

v1 whole, which is shorter than its diff:
```python
import functools

import jax
import jax.numpy as jnp
from jax import lax
from jax.experimental import pallas as pl
from jax.experimental.pallas import tpu as pltpu
from jax.sharding import PartitionSpec as P

D = 8192
HEADS = 64
HD = 128
V = 91
CH = 16
MESH = pl.DeviceIdType.MESH
F32 = jnp.float32
BF16 = jnp.bfloat16


def fallback_tail(grouped, attn, value_t, out_w, group_size):
    pooled = jnp.einsum("vth,vtd->thd", attn, grouped, preferred_element_type=F32).astype(BF16)
    own_tokens = pooled.shape[0]
    if group_size >= HEADS:
        spread = jnp.repeat(pooled, group_size // HEADS, axis=1)[:, :, None, :]
    else:
        spread = pooled.reshape(own_tokens, group_size, HEADS // group_size, D)
    received = lax.all_to_all(spread, "dev", split_axis=1, concat_axis=0, tiled=True)
    all_tokens = received.shape[0]
    head_share = received.shape[2]
    received = received.reshape(all_tokens, head_share, D)
    columns = value_t.shape[0]
    value_heads = jnp.einsum(
        "thd,hcd->thc",
        received,
        value_t.reshape(head_share, columns // head_share, D),
        preferred_element_type=F32,
    )
    value_heads = value_heads.reshape(all_tokens, columns).astype(BF16)
    summed = lax.psum_scatter(
        jnp.dot(value_heads, out_w, preferred_element_type=F32),
        "dev",
        scatter_dimension=0,
        tiled=True,
    )
    return summed.astype(BF16)


def softmax_slots(logits):
    slot = lax.broadcasted_iota(jnp.int32, logits.shape, 0)
    logits = jnp.where(slot < V, logits, -1e30)
    row_max = jnp.max(logits, axis=0, keepdims=True)
    weights = jnp.exp(logits - row_max)
    return (weights / jnp.sum(weights, axis=0, keepdims=True)).astype(BF16)


def tail_kernel(
    n, pix, w, var, attn, value_hbm, out_hbm, result,
    embf, pf, pool, got, vbuf, obuf, part, rc, r1, r2, ysum, rz, fbuf, gbuf,
    wsem, psend, precv, csend, crecv, s1send, s1recv, s2send, s2recv, zsend, zrecv, fsend, frecv,
):
    me = lax.axis_index("dev")
    core, x, y, z = me % 2, (me // 2) % 2, (me // 4) % 2, me // 8
    nz = n // 8
    slots, tokens, _ = pix.shape
    dl = w.shape[2]
    lanes = dl // 128
    hs = HEADS // n
    chunks = tokens // CH
    take = hs * CH
    load_v = pltpu.make_async_copy(value_hbm, vbuf, wsem.at[0])
    load_o = pltpu.make_async_copy(out_hbm, obuf, wsem.at[1])
    load_v.start()
    load_o.start()

    def embed_one(v, carry):
        e = jnp.dot(pix[v], w[v], preferred_element_type=F32) + var[v]
        e = e.astype(BF16).astype(F32)
        for k in range(lanes):
            embf[k, pl.ds(v, tokens, stride=slots), :] = e[:, k * 128:(k + 1) * 128]
        return carry

    lax.fori_loop(0, slots, embed_one, 0, unroll=4)

    def exchange(c, partner, slot):
        return pltpu.make_async_remote_copy(
            src_ref=pool.at[c, pl.ds(pl.multiple_of(partner * take, 16), take), :],
            dst_ref=got.at[slot, c],
            send_sem=psend.at[c, partner],
            recv_sem=precv.at[c, slot],
            device_id=(partner,),
            device_id_type=MESH,
        )

    for c in range(chunks):
        def pool_one(tt, carry, c=c):
            t = c * CH + tt
            row = pl.ds(pl.multiple_of(t * slots, 8), slots)
            em = jnp.concatenate([embf[k, row, :] for k in range(lanes)], axis=1).astype(BF16)
            p = lax.dot_general(attn[t], em, (((0,), (0,)), ((), ())), preferred_element_type=F32)
            for k in range(lanes):
                pf[k, pl.ds(tt, HEADS, stride=CH), :] = p[:, k * 128:(k + 1) * 128]
            return carry

        lax.fori_loop(0, CH, pool_one, 0, unroll=2)

        def pack(i, carry, c=c):
            rows = pl.ds(pl.multiple_of(i * 64, 64), 64)
            pool[c, rows, :] = jnp.concatenate([pf[k, rows, :] for k in range(lanes)], axis=1).astype(BF16)
            return carry

        lax.fori_loop(0, HEADS * CH // 64, pack, 0)
        got[me, c] = pool[c, pl.ds(pl.multiple_of(me * take, 16), take), :]

        def send(i, carry, c=c):
            exchange(c, (me + n // 2 + i) % n, me).start()
            return carry

        lax.fori_loop(0, n // 2, send, 0)
        lax.fori_loop(n // 2 + 1, n, send, 0)

    load_v.wait()

    def value_one(i, accs):
        s = (me + i) % n
        block = got[s]
        cols = pl.ds(pl.multiple_of(s * dl, 128), dl)
        new = []
        for h in range(hs):
            r = block[:, h * CH:(h + 1) * CH, :].reshape(tokens, dl)
            vv = vbuf[h * HD:(h + 1) * HD, cols]
            new.append(accs[h] + lax.dot_general(r, vv, (((1,), (1,)), ((), ())), preferred_element_type=F32))
        return tuple(new)

    def arrive_one(i, accs):
        s = (me + i) % n
        for c in range(chunks):
            pltpu.make_async_remote_copy(
                src_ref=got.at[s, c], dst_ref=got.at[s, c], send_sem=psend.at[c, s],
                recv_sem=precv.at[c, s], device_id=(s,), device_id_type=MESH,
            ).wait_recv()
        return value_one(i, accs)

    accs = value_one(0, tuple(jnp.zeros((tokens, HD), F32) for _ in range(hs)))
    accs = lax.fori_loop(1, n, arrive_one, accs)
    heads = jnp.concatenate(accs, axis=1).astype(BF16)

    load_o.wait()
    wide = D // 8
    half_w = wide // 2

    def out_blocks(cc, half):
        for a in range(2):
            for b in range(2):
                q = cc + 2 * (a if half == 0 else b) + 4 * (b if half == 0 else a)
                col = pl.multiple_of(q * wide + half * half_w, 128)
                part[cc, half, a, b] = jnp.dot(heads, obuf[:, pl.ds(col, half_w)], preferred_element_type=F32)

    def remote(src, dst, ss, rs, dev):
        return pltpu.make_async_remote_copy(
            src_ref=src, dst_ref=dst, send_sem=ss, recv_sem=rs, device_id=(dev,), device_id_type=MESH
        )

    other = me + 1 - 2 * core
    xn = me + 2 * (1 - 2 * x)
    yn = me + 4 * (1 - 2 * y)
    core_copies = []
    for half in range(2):
        out_blocks(1 - core, half)
        cp = remote(part.at[1 - core, half], rc.at[half], csend.at[half], crecv.at[half], other)
        cp.start()
        core_copies.append(cp)
    for half in range(2):
        out_blocks(core, half)
    first = (x, y)
    second = (y, x)
    first_dev = (xn, yn)
    second_dev = (yn, xn)
    stage1 = []
    for half in range(2):
        core_copies[half].wait_recv()
        away = 1 - first[half]
        for b in range(2):
            part[core, half, away, b] = part[core, half, away, b] + rc[half, away, b]
        cp = remote(part.at[core, half, away], r1.at[half], s1send.at[half], s1recv.at[half], first_dev[half])
        cp.start()
        stage1.append(cp)
    for half in range(2):
        own = first[half]
        for b in range(2):
            part[core, half, own, b] = part[core, half, own, b] + rc[half, own, b]
    stage2 = []
    for half in range(2):
        own = first[half]
        stage1[half].wait_recv()
        away = 1 - second[half]
        part[core, half, own, away] = part[core, half, own, away] + r1[half, away]
        cp = remote(part.at[core, half, own, away], r2.at[half], s2send.at[half], s2recv.at[half], second_dev[half])
        cp.start()
        stage2.append(cp)
    for half in range(2):
        own, mine = first[half], second[half]
        kept = part[core, half, own, mine] + r1[half, mine]
        stage2[half].wait_recv()
        ysum[half] = kept + r2[half]
    rows_z = tokens // nz
    zcopies = []
    for dz in range(1, nz):
        zz = (z + dz) % nz
        cp = remote(
            ysum.at[:, pl.ds(pl.multiple_of(zz * rows_z, 8), rows_z), :],
            rz.at[dz - 1], zsend.at[dz - 1], zrecv.at[dz - 1], me + 8 * (zz - z),
        )
        cp.start()
        zcopies.append(cp)
    total = ysum[:, pl.ds(pl.multiple_of(z * rows_z, 8), rows_z), :]
    for dz in range(1, nz):
        zcopies[dz - 1].wait_recv()
        total = total + rz[dz - 1]
    tok = tokens // n
    for k in range(8):
        for half in range(2):
            fbuf[k, :, half * half_w:(half + 1) * half_w] = total[half, k * tok:(k + 1) * tok, :]
    q = me % 8
    fcopies = []
    for dk in range(1, 8):
        k = (q + dk) % 8
        cp = remote(fbuf.at[k], gbuf.at[q], fsend.at[k], frecv.at[q], me - q + k)
        cp.start()
        fcopies.append(cp)
    gbuf[q] = fbuf[q]
    for dk in range(1, 8):
        k = (q + dk) % 8
        remote(gbuf.at[k], gbuf.at[k], fsend.at[k], frecv.at[k], me - q + k).wait_recv()
    for k in range(8):
        result[:, k * wide:(k + 1) * wide] = gbuf[k].astype(BF16)

    for group in (core_copies, stage1, stage2, zcopies, fcopies):
        for cp in group:
            cp.wait_send()

    def drain(i, carry):
        for c in range(chunks):
            exchange(c, (me + i) % n, me).wait_send()
        return carry

    lax.fori_loop(1, n, drain, 0)


def fused_tail(n, pix, w, var, attn, value_t, out_w):
    slots, tokens, _ = pix.shape
    dl = w.shape[2]
    lanes = dl // 128
    hs = HEADS // n
    chunks = tokens // CH
    nz = n // 8
    wide = D // 8
    half_w = wide // 2
    tok = tokens // n
    dma = pltpu.SemaphoreType.DMA
    vmem = pl.BlockSpec(memory_space=pltpu.VMEM)
    hbm = pl.BlockSpec(memory_space=pl.ANY)
    return pl.pallas_call(
        functools.partial(tail_kernel, n),
        out_shape=jax.ShapeDtypeStruct((tok, D), BF16),
        in_specs=[vmem] * 4 + [hbm] * 2,
        out_specs=vmem,
        scratch_shapes=[
            pltpu.VMEM((lanes, tokens * slots, 128), F32),
            pltpu.VMEM((lanes, HEADS * CH, 128), F32),
            pltpu.VMEM((chunks, HEADS * CH, dl), BF16),
            pltpu.VMEM((n, chunks, hs * CH, dl), BF16),
            pltpu.VMEM(value_t.shape, BF16),
            pltpu.VMEM(out_w.shape, BF16),
            pltpu.VMEM((2, 2, 2, 2, tokens, half_w), F32),
            pltpu.VMEM((2, 2, 2, tokens, half_w), F32),
            pltpu.VMEM((2, 2, tokens, half_w), F32),
            pltpu.VMEM((2, tokens, half_w), F32),
            pltpu.VMEM((2, tokens, half_w), F32),
            pltpu.VMEM((nz - 1, 2, tokens // nz, half_w), F32),
            pltpu.VMEM((8, tok, wide), F32),
            pltpu.VMEM((8, tok, wide), F32),
            dma((2,)), dma((chunks, n)), dma((chunks, n)),
            dma((2,)), dma((2,)), dma((2,)), dma((2,)), dma((2,)), dma((2,)),
            dma((nz - 1,)), dma((nz - 1,)), dma((8,)), dma((8,)),
        ],
        compiler_params=pltpu.CompilerParams(
            has_side_effects=True, vmem_limit_bytes=60 * 1024 * 1024
        ),
    )(pix, w, var, attn, value_t, out_w)


def body(pixels, embed_w, var_embed, key_w, query, value_t, out_w):
    n = lax.axis_size("dev")
    own_slots, tokens, _ = pixels.shape
    own_embed = jnp.einsum("vtp,vpd->vtd", pixels, embed_w, preferred_element_type=F32)
    own_embed = (own_embed + var_embed.astype(F32)[:, None, :]).astype(BF16)
    key_rows = key_w.shape[0]
    keyq_part = jnp.einsum(
        "dhj,hj->dh",
        key_w.astype(F32).reshape(key_rows, HEADS, HD),
        query.reshape(HEADS, HD),
        precision=lax.Precision.HIGHEST,
    )
    keyq = lax.all_gather(keyq_part, "dev", axis=0, tiled=True)
    scale = jnp.sqrt(F32(HD))
    if n % 8 or n // 8 < 2 or HEADS % n or D // n % 128 or tokens % (8 * (n // 8)) or tokens % CH:
        grouped = lax.all_to_all(own_embed, "dev", split_axis=1, concat_axis=0, tiled=True)
        logits = jnp.einsum(
            "vtd,dh->vth", grouped.astype(F32), keyq, precision=lax.Precision.HIGHEST
        ) / scale
        return fallback_tail(grouped, softmax_slots(logits), value_t, out_w, n)
    weights = jnp.concatenate([embed_w, var_embed[:, None, :]], axis=1)
    weights = lax.all_to_all(weights, "dev", split_axis=2, concat_axis=0, tiled=True)
    all_pixels = lax.all_gather(pixels, "dev", axis=0, tiled=True)
    own_logits = jnp.einsum(
        "vtd,dh->vth", own_embed.astype(F32), keyq, precision=lax.Precision.HIGHEST
    ) / scale
    logits = lax.all_gather(own_logits, "dev", axis=0, tiled=True)
    attn = jnp.swapaxes(softmax_slots(logits), 0, 1)
    patch = pixels.shape[2]
    return fused_tail(
        n, all_pixels, weights[:, :patch, :], weights[:, patch:, :].astype(F32), attn, value_t, out_w
    )


def solution(mesh):
    placed = (
        P("dev", None, None),
        P("dev", None, None),
        P("dev", None),
        P("dev", None),
        P(),
        P("dev", None),
        P("dev", None),
    )
    return jax.shard_map(
        body, mesh=mesh, in_specs=placed, out_specs=P("dev", None), check_vma=False
    )
```

time: 286 us -> 318 us (1.11)
  Pallas kernels: 0 us -> 92 us
  waiting for transfers between devices: 142 us -> 55.5 us
  local copies, waits for them, and re-layouts: 30 us -> 65.7 us
  other arithmetic: 1.12 us -> 23.6 us
  matrix products: 25.6 us -> 10.9 us
  blocking collectives: 61.8 us -> 51.5 us
  starting transfers between devices: 11.6 us -> 3.95 us
    all_to_all x2 -> x1, waiting for transfers between devices: 142 us -> 0.01 us  [body(): lax.all_to_all(weights, 'dev', split_axis=2, concat_axis=0, tiled=True)]
    pallas_call x0 -> x1, Pallas kernels: none -> 92 us  [fused_tail(): pl.pallas_call(functools.partial(tail_kernel, n), out_shape=jax.ShapeDtyp...]
    unnamed x1 -> x0, blocking collectives: 61.8 us -> none
    all_gather x1, waiting for transfers between devices: 0.01 us -> 55.4 us  [body(): keyq = lax.all_gather(keyq_part, 'dev', axis=0, tiled=True)]
    all_gather x0 -> x1, blocking collectives: none -> 51.5 us  [body(): all_pixels = lax.all_gather(pixels, 'dev', axis=0, tiled=True)]
    unnamed x6 -> x14, local copies, waits for them, and re-layouts: 0.24 us -> 36.9 us
    dot_general x6 -> x3, matrix products: 25.6 us -> 10.9 us  [the longest x1 4.82 us: body(): jnp.einsum('vtd,dh->vth', own_embed.astype(F32), keyq, precision=lax.Prec...]
    unnamed x0 -> x1, other arithmetic: none -> 14.1 us
  transfers between devices with their start and end apart: 3 -> 3, of which waited for: 2 -> 1; matrix products, arithmetic and copies ran while one was open for 7% -> 23% of each run, Pallas kernels for 0% -> 0%
where the time goes in v1:
time: 318 us; the launch traced here: 317 us
  Pallas kernels  92 us (29%)
  local copies, waits for them, and re-layouts  65.7 us (21%)
  waiting for transfers between devices  55.5 us (17%)
  blocking collectives  51.5 us (16%)
  other arithmetic  23.6 us (7%)
  between operations  13.5 us (4%)
  matrix products  10.9 us (3%)
  starting transfers between devices  3.95 us (1%)
    pallas_call x1, Pallas kernels, fused_tail(): pl.pallas_call(functools.partial(tail_kernel, n), out_shape=jax.ShapeDtyp...  92 us
    all_gather x1, waiting for transfers between devices, body(): keyq = lax.all_gather(keyq_part, 'dev', axis=0, tiled=True)  55.4 us
    all_gather x1, blocking collectives, body(): all_pixels = lax.all_gather(pixels, 'dev', axis=0, tiled=True)  51.5 us
    unnamed x14, local copies, waits for them, and re-layouts  36.9 us
    unnamed x1, other arithmetic  14.1 us
    all_to_all x1, local copies, waits for them, and re-layouts, body(): lax.all_to_all(weights, 'dev', split_axis=2, concat_axis=0, tiled=True)  10.9 us
    broadcast_in_dim x1, local copies, waits for them, and re-layouts, body(): weights = jnp.concatenate([embed_w, var_embed[:, None, :]], axis=1)  8.43 us
    reshape x1, local copies, waits for them, and re-layouts, body(): key_w.astype(F32).reshape(key_rows, HEADS, HD)  6.36 us
  transfers between devices with their start and end apart: 3, of which 1 were waited for; matrix products, arithmetic and copies ran while one was open for 23% of the time, Pallas kernels for 0%

profile of v1, /device:TPU:0, one launch (start us, length us, event | category | flops | bytes accessed | tf_op | source)
XLA Modules:
  0.0 316.6 jit_solution(2448766277330998266)
XLA Ops:
  6.5 0.0 copy-start
  6.5 0.0 all-gather.3.cloned.1.call-start
  6.5 6.4 %copy.35 = bf16[256,8192]{0,1:T(8,128)(2,1)} copy(bf16[256,8192]{1,0:T(8,128)(2,1)} %param.10) | data formatting | bytes 8388608 | tf_op jit(solution)/shard_map/reshape | solution.py:300
  12.9 0.0 copy-start.3
  12.9 0.0 copy-start.4
  12.9 0.0 copy-done
  12.9 3.9 %fusion.16 = f32[64,1,256]{2,1,0:T(1,128)S(1)} fusion(f32[64,128,1]{1,2,0:T(1,128)S(1)} %bitcast.31, bf16[256,64,128]{0,2,1:T(8,128)(2,1)} %bitcast.33), kind=kOutput, calls=%fused_computation.22 | convolution fusion | flops 25165824 | bytes 4292608 | tf_op jit(solution)/shard_map/dhj,hj->dh/dot_general | solution.py:298
  16.9 0.6 copy.46
  17.5 0.0 all-gather.3.cloned.1.call-update
  17.5 0.0 all-gather.5.cloned.1.call-start
  17.6 0.0 copy-done.3
  17.6 0.0 copy-done.4
  17.6 2.2 fusion.2
  19.8 55.4 %all-gather.3.cloned.1.call-done = f32[8192,64]{0,1:T(8,128)} async-done(((f32[256,64]{0,1:T(8,128)}), f32[8192,64]{0,1:T(8,128)}) %all-gather.3.cloned.1.call-update) | async-done | bytes 2097168 | tf_op jit(solution)/shard_map/all_gather | solution.py:304
  75.2 4.8 %fusion.9 = f32[3,64,64]{2,1,0:T(8,128)} fusion(bf16[3,64,8192]{2,1,0:T(8,128)(2,1)S(1)} %fusion.2, f32[8192,64]{0,1:T(8,128)} %all-gather.3.cloned.1.call-done), kind=kOutput, calls=%fused_computation.14 | convolution fusion | flops 1207971840 | bytes 5292032 | tf_op jit(solution)/shard_map/vtd,dh->vth/dot_general | solution.py:315
  80.0 0.0 all-gather.5.cloned.1.call-update
  80.1 10.0 %copy.27 = bf16[3,16,8192]{1,0,2:T(4,128)(2,1)} copy(bf16[3,16,8192]{2,1,0:T(8,128)(2,1)} %param.8) | data formatting | bytes 1572864 | tf_op args[1]
  90.0 8.4 %copy.28 = bf16[3,1,8192]{1,0,2:T(4,128)(2,1)} copy(bf16[3,1,8192]{2,0,1:T(4,128)(2,1)S(1)} %bitcast.36) | data formatting | bytes 98304 | tf_op jit(solution)/shard_map/broadcast_in_dim | solution.py:312
  98.5 14.1 %fusion.15 = bf16[8192,3,17]{2,1,0:T(4,128)(2,1)} fusion(bf16[3,1,8192]{1,0,2:T(4,128)(2,1)} %copy.28, bf16[3,16,8192]{1,0,2:T(4,128)(2,1)} %copy.27), kind=kLoop, calls=%fused_computation.21 | loop fusion | flops 1671168 | bytes 1671168
  112.5 14.5 %reshape.14 = bf16[32,2,6528]{2,1,0:T(2,128)(2,1)} reshape(bf16[8192,3,17]{2,1,0:T(4,128)(2,1)} %fusion.15) | data formatting | bytes 1671168
  127.0 3.9 %all-to-all-start = ((bf16[32,2,6528]{2,1,0:T(2,128)(2,1)}), bf16[32,2,6528]{2,1,0:T(2,128)(2,1)S(1)}, u32[]{:S(2)}, u32[]{:S(2)}) async-start(bf16[32,2,6528]{2,1,0:T(2,128)(2,1)} %reshape.14), calls=%async_computation | async-start | bytes 1671168 | tf_op jit(solution)/shard_map/all_to_all | solution.py:313
  130.9 51.5 %all_gather.9 = bf16[96,64,16]{1,2,0:T(8,128)(2,1)S(1)} all-gather(bf16[3,64,16]{1,2,0:T(8,128)(2,1)S(1)} %copy-done.4), channel_id=1, replica_groups=mesh['dev'=32] {'dev'}, dimensions={0}, use_global_device_ids=true | all-gather | bytes 202752 | tf_op jit(solution)/shard_map/all_gather | solution.py:314
  182.4 1.5 copy.31.pix
  183.9 0.0 all-to-all-done
  183.9 11.0 %reshape.15 = bf16[8192,3,17]{2,1,0:T(4,128)(2,1)} reshape(bf16[32,2,6528]{2,1,0:T(2,128)(2,1)S(1)} %all-to-all-done) | data formatting | bytes 1671168
  194.9 10.9 %copy.29 = bf16[3,17,32,256]{3,1,0,2:T(8,128)(2,1)S(1)} copy(bf16[3,17,32,256]{1,0,3,2:T(4,128)(2,1)} %bitcast.32) | data formatting | bytes 1671168 | tf_op jit(solution)/shard_map/all_to_all | solution.py:313
  205.9 0.9 slice.8.w
  206.8 0.7 slice_convert_fusion.var
  207.5 0.0 all-gather.5.cloned.1.call-done
  207.5 0.0 copy-start.2
  207.5 4.6 %fusion.1 = f32[96,64,64]{2,0,1:T(8,128)S(1)} fusion(f32[96,64,64]{2,1,0:T(8,128)} %all-gather.5.cloned.1.call-done, pred[96]{0:T(512)(128)(4,1)S(1)} %iota_compare_fusion), kind=kOutput, calls=%fused_computation.1 | output fusion | flops 397407 | bytes 3145824 | tf_op jit(solution)/shard_map/sub | solution.py:52
  212.1 0.0 copy-done.2
  212.1 0.0 copy-start.1
  212.1 4.3 %fusion.8.attn = bf16[64,96,64]{2,1,0:T(8,128)(2,1)} fusion(f32[96,64,64]{2,0,1:T(8,128)S(1)} %fusion.1, f32[96,64,64]{2,1,0:T(8,128)S(1)} %copy-done.2, pred[96]{0:T(512)(128)(4,1)S(1)} %iota_compare_fusion), kind=kOutput, calls=%fused_computation.13 | output fusion | flops 1577055 | bytes 3932256 | tf_op jit(solution)/shard_map/div | solution.py:53
  216.4 92.0 %shard_map.73 = bf16[2,8192]{1,0:T(2,128)(2,1)} custom-call(bf16[96,64,16]{2,1,0:T(8,128)(2,1)} %copy.31.pix, bf16[96,16,256]{2,1,0:T(8,128)(2,1)} %slice.8.w, f32[96,1,256]{2,1,0:T(1,128)} %slice_convert_fusion.var, bf16[64,96,64]{2,1,0:T(8,128)(2,1)} %fusion.8.attn, bf16[256,8192]{1,0:T(8,128)(2,1)} %value_hbm.1, bf16[256,8192]{1,0:T(8,128)(2,1)} %out_hbm.1), custom_call_target="tpu_custom_call" | custom-call | tf_op jit(solution)/shard_map/pallas_call | solution.py:262
  308.4 1.4 copy.48
  309.8 0.0 copy-done.1
  (2 shorter events, 0.0 us)
Async XLA Ops:
  6.5 6.4 %copy-start = (f32[8192]{0:T(1024)S(1)}, f32[8192]{0:T(1024)}, u32[]{:S(2)}) copy-start(f32[8192]{0:T(1024)} %param.11) | copy-start | bytes 98308
  6.5 68.7 %all-gather.3.cloned.1.call-start = ((), (), s32[]{:S(2)}) async-start(), calls=%async_computation.1 | async-start | bytes 2162688 | tf_op jit(solution)/shard_map/all_gather | solution.py:304
  12.9 4.7 %copy-start.3 = (bf16[3,8192]{1,0:T(4,128)(2,1)S(1)}, bf16[3,8192]{1,0:T(4,128)(2,1)}, u32[]{:S(2)}) copy-start(bf16[3,8192]{1,0:T(4,128)(2,1)} %param.9) | copy-start | bytes 147460
  12.9 4.7 %copy-start.4 = (bf16[3,64,16]{1,2,0:T(8,128)(2,1)S(1)}, bf16[3,64,16]{1,2,0:T(8,128)(2,1)}, u32[]{:S(2)}) copy-start(bf16[3,64,16]{1,2,0:T(8,128)(2,1)} %param.7) | copy-start | bytes 18436
  17.5 190.0 %all-gather.5.cloned.1.call-start = ((), (), s32[]{:S(2)}) async-start(), calls=%async_computation.2 | async-start | bytes 3244032 | tf_op jit(solution)/shard_map/all_gather | solution.py:318
  127.0 56.9 %all-to-all-start = ((bf16[32,2,6528]{2,1,0:T(2,128)(2,1)}), bf16[32,2,6528]{2,1,0:T(2,128)(2,1)S(1)}, u32[]{:S(2)}, u32[]{:S(2)}) async-start(bf16[32,2,6528]{2,1,0:T(2,128)(2,1)} %reshape.14), calls=%async_computation | async-start | bytes 1671168 | tf_op jit(solution)/shard_map/all_to_all | solution.py:313
  207.5 4.6 %copy-start.2 = (f32[96,64,64]{2,1,0:T(8,128)S(1)}, f32[96,64,64]{2,1,0:T(8,128)}, u32[]{:S(2)}) copy-start(f32[96,64,64]{2,1,0:T(8,128)} %all-gather.5.cloned.1.call-done) | copy-start | bytes 4718596
  212.1 97.7 %copy-start.1 = (f32[8192]{0:T(1024)S(1)}, f32[8192]{0:T(1024)}, u32[]{:S(2)}) copy-start(f32[8192]{0:T(1024)} %param.11) | copy-start | bytes 98308
Sparse Core Ops, SparseCore 0:
  17.6 57.5 all-gather.2
  80.2 59.4 all-gather.4

commit v2 on v1

--- a/solution.py
+++ b/solution.py
@@ -12,74 +12,199 @@
 HD = 128
 V = 91
 CH = 16
+EARLY = 8
 MESH = pl.DeviceIdType.MESH
 F32 = jnp.float32
 BF16 = jnp.bfloat16
 
 
-def fallback_tail(grouped, attn, value_t, out_w, group_size):
-    pooled = jnp.einsum("vth,vtd->thd", attn, grouped, preferred_element_type=F32).astype(BF16)
-    own_tokens = pooled.shape[0]
-    if group_size >= HEADS:
-        spread = jnp.repeat(pooled, group_size // HEADS, axis=1)[:, :, None, :]
-    else:
-        spread = pooled.reshape(own_tokens, group_size, HEADS // group_size, D)
-    received = lax.all_to_all(spread, "dev", split_axis=1, concat_axis=0, tiled=True)
-    all_tokens = received.shape[0]
-    head_share = received.shape[2]
-    received = received.reshape(all_tokens, head_share, D)
-    columns = value_t.shape[0]
-    value_heads = jnp.einsum(
-        "thd,hcd->thc",
-        received,
-        value_t.reshape(head_share, columns // head_share, D),
-        preferred_element_type=F32,
-    )
-    value_heads = value_heads.reshape(all_tokens, columns).astype(BF16)
-    summed = lax.psum_scatter(
-        jnp.dot(value_heads, out_w, preferred_element_type=F32),
-        "dev",
-        scatter_dimension=0,
-        tiled=True,
-    )
-    return summed.astype(BF16)
-
-
-def softmax_slots(logits):
-    slot = lax.broadcasted_iota(jnp.int32, logits.shape, 0)
-    logits = jnp.where(slot < V, logits, -1e30)
-    row_max = jnp.max(logits, axis=0, keepdims=True)
-    weights = jnp.exp(logits - row_max)
-    return (weights / jnp.sum(weights, axis=0, keepdims=True)).astype(BF16)
+def remote(src, dst, ss, rs, dev):
+    return pltpu.make_async_remote_copy(
+        src_ref=src, dst_ref=dst, send_sem=ss, recv_sem=rs, device_id=(dev,), device_id_type=MESH
+    )
+
+
+def slot_of(s, nz):
+    return (s % 2 * 4 + (s // 4) % 2 * 2 + (s // 2) % 2) * nz + s // 8
+
+
+def gather_steps(buf, send, recv, me, nz):
+    core, x, y, z = me % 2, (me // 2) % 2, (me // 4) % 2, me // 8
+    q, qx, qy, qd = (
+        core * 4 + yy * 2 + xx for yy, xx in ((y, x), (y, 1 - x), (1 - y, x), (1 - y, 1 - x))
+    )
+    xn, yn, other = me + 2 * (1 - 2 * x), me + 4 * (1 - 2 * y), me + 1 - 2 * core
+    started = []
+
+    def go(k, block, dev):
+        cp = remote(block, block, send.at[k], recv.at[k], dev)
+        cp.start()
+        started.append(cp)
+        return cp
+
+    def along_z():
+        for dz in range(1, nz):
+            go(dz - 1, buf.at[q * nz + z], me + 8 * ((z + dz) % nz - z))
+
+    def rest():
+        for dz in range(1, nz):
+            started[dz - 1].wait_recv()
+        k = nz - 1
+        half = nz // 2
+        own = buf.at[pl.ds(q * nz, nz)]
+        cx = go(k, own, xn)
+        cy = go(k + 1, own, yn)
+        c0 = go(k + 2, own, other)
+        cx.wait_recv()
+        fy = go(k + 3, buf.at[pl.ds(qx * nz, half)], yn)
+        c1 = go(k + 5, buf.at[pl.ds(qx * nz, nz)], other)
+        cy.wait_recv()
+        fx = go(k + 4, buf.at[pl.ds(qy * nz + half, nz - half)], xn)
+        c2 = go(k + 6, buf.at[pl.ds(qy * nz, nz)], other)
+        return fy, fx, c0, c1, c2
+
+    def finish(fy, fx, c0, c1, c2):
+        fy.wait_recv()
+        fx.wait_recv()
+        c3 = go(nz + 6, buf.at[pl.ds(qd * nz, nz)], other)
+        for cp in (c0, c1, c2, c3):
+            cp.wait_recv()
+        for cp in started:
+            cp.wait_send()
+
+    return along_z, rest, finish
 
 
 def tail_kernel(
-    n, pix, w, var, attn, value_hbm, out_hbm, result,
+    n, pix, wp, var, qtile, key_hbm, value_hbm, out_hbm, result,
+    kbuf, kq, wall, vall, oemb, lg, prob,
     embf, pf, pool, got, vbuf, obuf, part, rc, r1, r2, ysum, rz, fbuf, gbuf,
+    gsend, grecv, hsend, hrecv, wsnd, wrcv, vsnd, vrcv, ksem,
     wsem, psend, precv, csend, crecv, s1send, s1recv, s2send, s2recv, zsend, zrecv, fsend, frecv,
 ):
     me = lax.axis_index("dev")
     core, x, y, z = me % 2, (me // 2) % 2, (me // 4) % 2, me // 8
     nz = n // 8
-    slots, tokens, _ = pix.shape
-    dl = w.shape[2]
+    vs, tokens, patch = pix.shape
+    slots = n * vs
+    dl = D // n
     lanes = dl // 128
     hs = HEADS // n
     chunks = tokens // CH
     take = hs * CH
+    ht = tokens // 2
+    mine = slot_of(me, nz)
+    load_k = pltpu.make_async_copy(key_hbm, kbuf, ksem.at[0])
+    load_k.start()
     load_v = pltpu.make_async_copy(value_hbm, vbuf, wsem.at[0])
     load_o = pltpu.make_async_copy(out_hbm, obuf, wsem.at[1])
+
+    def cols_of(s):
+        return pl.ds(pl.multiple_of(s * dl, 128), dl)
+
+    def w_copy(partner, src):
+        return remote(wp.at[:, :, cols_of(partner)], wall.at[src], wsnd.at[partner], wrcv.at[src], partner)
+
+    def v_copy(partner, src):
+        return remote(var.at[:, :, cols_of(partner)], vall.at[src], vsnd.at[partner], vrcv.at[src], partner)
+
+    def w_send(i, carry):
+        partner = (me + n // 2 + i) % n
+        w_copy(partner, me).start()
+        v_copy(partner, me).start()
+        return carry
+
+    early = EARLY
+    lax.fori_loop(0, early, w_send, 0)
+    load_k.wait()
     load_v.start()
     load_o.start()
-
-    def embed_one(v, carry):
-        e = jnp.dot(pix[v], w[v], preferred_element_type=F32) + var[v]
-        e = e.astype(BF16).astype(F32)
-        for k in range(lanes):
-            embf[k, pl.ds(v, tokens, stride=slots), :] = e[:, k * 128:(k + 1) * 128]
+    for kt in range(HEADS // 2):
+        r = lax.dot_general(
+            qtile[kt], kbuf[:, kt * 2 * HD:(kt + 1) * 2 * HD], (((1,), (1,)), ((), ())),
+            preferred_element_type=F32,
+        )
+        kq[mine, 2 * kt:2 * kt + 2, :] = r[0:2] + r[2:4] + r[4:6]
+    kq_z, kq_rest, kq_finish = gather_steps(kq, gsend, grecv, me, nz)
+    lg_z, lg_rest, lg_finish = gather_steps(lg, hsend, hrecv, me, nz)
+    kq_z()
+
+    def own_one(s, carry):
+        cols = cols_of(s)
+        for v in range(vs):
+            e = jnp.dot(pix[v], wp[v, :, cols], preferred_element_type=F32) + var[v, :, cols]
+            oemb[v * tokens:(v + 1) * tokens, cols] = e.astype(BF16)
         return carry
 
-    lax.fori_loop(0, slots, embed_one, 0, unroll=4)
+    lax.fori_loop(0, n // 2, own_one, 0)
+    state = kq_rest()
+    lax.fori_loop(n // 2, n, own_one, 0)
+    wall[me] = wp[:, :, cols_of(me)]
+    vall[me] = var[:, :, cols_of(me)]
+    kq_finish(*state)
+    lax.fori_loop(early, n // 2, w_send, 0)
+    lax.fori_loop(n // 2 + 1, n, w_send, 0)
+
+    def logit_one(s, acc):
+        a = kq[slot_of(s, nz)]
+        hi = a.astype(BF16)
+        rest = a - hi.astype(F32)
+        mid = rest.astype(BF16)
+        low = (rest - mid.astype(F32)).astype(BF16)
+        b = jnp.concatenate([hi, mid, low], axis=0)
+        return acc + lax.dot_general(
+            oemb[:, cols_of(s)], b, (((1,), (1,)), ((), ())), preferred_element_type=F32
+        )
+
+    acc = lax.fori_loop(0, n, logit_one, jnp.zeros((vs * tokens, 3 * HEADS), F32))
+    logit = (acc[:, :HEADS] + acc[:, HEADS:2 * HEADS] + acc[:, 2 * HEADS:]) / jnp.sqrt(F32(HD))
+    for v in range(vs):
+        pair = jnp.concatenate(
+            [logit[v * tokens:v * tokens + ht], logit[v * tokens + ht:(v + 1) * tokens]], axis=1
+        )
+        live = jnp.full(pair.shape, me * vs + v, jnp.int32) < V
+        lg[mine, v * ht:(v + 1) * ht, :] = jnp.where(live, pair, -1e30)
+    lg_z()
+
+    def embed_one(s):
+        ps = jnp.transpose(wall[s, vs].astype(F32)).astype(BF16)
+        at = slot_of(s, nz) * vs
+        for v in range(vs):
+            e = jnp.dot(ps[v * tokens:(v + 1) * tokens], wall[s, v], preferred_element_type=F32) + vall[s, v]
+            e = e.astype(BF16).astype(F32)
+            for k in range(lanes):
+                embf[k, pl.ds(at + v, tokens, stride=slots), :] = e[:, k * 128:(k + 1) * 128]
+
+    def arrive_w(i, carry):
+        s = (me + i) % n
+        w_copy(s, s).wait_recv()
+        v_copy(s, s).wait_recv()
+        embed_one(s)
+        return carry
+
+    embed_one(me)
+    state = lg_rest()
+    lax.fori_loop(1, n, arrive_w, 0)
+    lg_finish(*state)
+    for g in range(ht // 8):
+        def at_v(v, g=g):
+            return lg[v // vs, pl.ds(pl.multiple_of(v % vs * ht + g * 8, 8), 8), :]
+
+        top = lax.fori_loop(1, slots, lambda v, m: jnp.maximum(m, at_v(v)), at_v(0), unroll=4)
+
+        def exp_one(v, total, g=g, at_v=at_v, top=top):
+            e = jnp.exp(at_v(v) - top)
+            prob[pl.ds(pl.multiple_of(v * ht + g * 8, 8), 8), :] = e
+            return total + e
+
+        total = lax.fori_loop(0, slots, exp_one, jnp.zeros((8, 128), F32), unroll=4)
+
+        def div_one(v, carry, g=g, total=total):
+            rows = pl.ds(pl.multiple_of(v * ht + g * 8, 8), 8)
+            prob[rows, :] = prob[rows, :] / total
+            return carry
+
+        lax.fori_loop(0, slots, div_one, 0, unroll=4)
 
     def exchange(c, partner, slot):
         return pltpu.make_async_remote_copy(
@@ -93,15 +218,20 @@
 
     for c in range(chunks):
         def pool_one(tt, carry, c=c):
-            t = c * CH + tt
-            row = pl.ds(pl.multiple_of(t * slots, 8), slots)
-            em = jnp.concatenate([embf[k, row, :] for k in range(lanes)], axis=1).astype(BF16)
-            p = lax.dot_general(attn[t], em, (((0,), (0,)), ((), ())), preferred_element_type=F32)
-            for k in range(lanes):
-                pf[k, pl.ds(tt, HEADS, stride=CH), :] = p[:, k * 128:(k + 1) * 128]
+            t = c * (CH // 2) + tt
+            at = prob[pl.ds(t, slots, stride=ht), :].astype(BF16)
+            for side in range(2):
+                row = pl.ds(pl.multiple_of((t + side * ht) * slots, 8), slots)
+                em = jnp.concatenate([embf[k, row, :] for k in range(lanes)], axis=1).astype(BF16)
+                p = lax.dot_general(
+                    at[:, side * HEADS:(side + 1) * HEADS], em, (((0,), (0,)), ((), ())),
+                    preferred_element_type=F32,
+                )
+                for k in range(lanes):
+                    pf[k, pl.ds(tt + side * (CH // 2), HEADS, stride=CH), :] = p[:, k * 128:(k + 1) * 128]
             return carry
 
-        lax.fori_loop(0, CH, pool_one, 0, unroll=2)
+        lax.fori_loop(0, CH // 2, pool_one, 0, unroll=2)
 
         def pack(i, carry, c=c):
             rows = pl.ds(pl.multiple_of(i * 64, 64), 64)
@@ -142,7 +272,11 @@
 
     accs = value_one(0, tuple(jnp.zeros((tokens, HD), F32) for _ in range(hs)))
     accs = lax.fori_loop(1, n, arrive_one, accs)
-    heads = jnp.concatenate(accs, axis=1).astype(BF16)
+    heads = jnp.concatenate(accs, axis=1)
+    hc = CH // 2
+    heads = jnp.concatenate(
+        [heads[c * CH + side * hc:c * CH + (side + 1) * hc] for side in range(2) for c in range(chunks)], axis=0
+    ).astype(BF16)
 
     load_o.wait()
     wide = D // 8
@@ -154,11 +288,6 @@
                 q = cc + 2 * (a if half == 0 else b) + 4 * (b if half == 0 else a)
                 col = pl.multiple_of(q * wide + half * half_w, 128)
                 part[cc, half, a, b] = jnp.dot(heads, obuf[:, pl.ds(col, half_w)], preferred_element_type=F32)
-
-    def remote(src, dst, ss, rs, dev):
-        return pltpu.make_async_remote_copy(
-            src_ref=src, dst_ref=dst, send_sem=ss, recv_sem=rs, device_id=(dev,), device_id_type=MESH
-        )
 
     other = me + 1 - 2 * core
     xn = me + 2 * (1 - 2 * x)
@@ -198,8 +327,8 @@
         cp.start()
         stage2.append(cp)
     for half in range(2):
-        own, mine = first[half], second[half]
-        kept = part[core, half, own, mine] + r1[half, mine]
+        own, kept_b = first[half], second[half]
+        kept = part[core, half, own, kept_b] + r1[half, kept_b]
         stage2[half].wait_recv()
         ysum[half] = kept + r2[half]
     rows_z = tokens // nz
@@ -241,14 +370,17 @@
     def drain(i, carry):
         for c in range(chunks):
             exchange(c, (me + i) % n, me).wait_send()
+        w_copy((me + i) % n, me).wait_send()
+        v_copy((me + i) % n, me).wait_send()
         return carry
 
     lax.fori_loop(1, n, drain, 0)
 
 
-def fused_tail(n, pix, w, var, attn, value_t, out_w):
-    slots, tokens, _ = pix.shape
-    dl = w.shape[2]
+def fused_tail(n, pix, wp, var, qtile, key_w, value_t, out_w):
+    vs, tokens, patch = pix.shape
+    slots = vs * n
+    dl = D // n
     lanes = dl // 128
     hs = HEADS // n
     chunks = tokens // CH
@@ -262,9 +394,16 @@
     return pl.pallas_call(
         functools.partial(tail_kernel, n),
         out_shape=jax.ShapeDtypeStruct((tok, D), BF16),
-        in_specs=[vmem] * 4 + [hbm] * 2,
+        in_specs=[vmem] * 4 + [hbm] * 3,
         out_specs=vmem,
         scratch_shapes=[
+            pltpu.VMEM(key_w.shape, BF16),
+            pltpu.VMEM((n, HEADS, dl), F32),
+            pltpu.VMEM((n, vs + 1, patch, dl), BF16),
+            pltpu.VMEM((n, vs, 1, dl), F32),
+            pltpu.VMEM((vs * tokens, D), BF16),
+            pltpu.VMEM((n, vs * tokens // 2, 2 * HEADS), F32),
+            pltpu.VMEM((slots * tokens // 2, 2 * HEADS), F32),
             pltpu.VMEM((lanes, tokens * slots, 128), F32),
             pltpu.VMEM((lanes, HEADS * CH, 128), F32),
             pltpu.VMEM((chunks, HEADS * CH, dl), BF16),
@@ -279,6 +418,8 @@
             pltpu.VMEM((nz - 1, 2, tokens // nz, half_w), F32),
             pltpu.VMEM((8, tok, wide), F32),
             pltpu.VMEM((8, tok, wide), F32),
+            dma((nz + 7,)), dma((nz + 7,)), dma((nz + 7,)), dma((nz + 7,)),
+            dma((n,)), dma((n,)), dma((n,)), dma((n,)), dma((1,)),
             dma((2,)), dma((chunks, n)), dma((chunks, n)),
             dma((2,)), dma((2,)), dma((2,)), dma((2,)), dma((2,)), dma((2,)),
             dma((nz - 1,)), dma((nz - 1,)), dma((8,)), dma((8,)),
@@ -286,41 +427,80 @@
         compiler_params=pltpu.CompilerParams(
             has_side_effects=True, vmem_limit_bytes=60 * 1024 * 1024
         ),
-    )(pix, w, var, attn, value_t, out_w)
-
-
-def body(pixels, embed_w, var_embed, key_w, query, value_t, out_w):
-    n = lax.axis_size("dev")
-    own_slots, tokens, _ = pixels.shape
-    own_embed = jnp.einsum("vtp,vpd->vtd", pixels, embed_w, preferred_element_type=F32)
-    own_embed = (own_embed + var_embed.astype(F32)[:, None, :]).astype(BF16)
+    )(pix, wp, var, qtile, key_w, value_t, out_w)
+
+
+def plain_body(pixels, embed_w, var_embed, key_w, query, value_t, out_w):
+    group_size = lax.axis_size("dev")
+    own_embed = jnp.einsum("vtp,vpd->vtd", pixels, embed_w, preferred_element_type=jnp.float32)
+    own_embed = (own_embed + var_embed.astype(jnp.float32)[:, None, :]).astype(jnp.bfloat16)
+    grouped = lax.all_to_all(own_embed, "dev", split_axis=1, concat_axis=0, tiled=True)
     key_rows = key_w.shape[0]
     keyq_part = jnp.einsum(
         "dhj,hj->dh",
-        key_w.astype(F32).reshape(key_rows, HEADS, HD),
+        key_w.astype(jnp.float32).reshape(key_rows, HEADS, HD),
         query.reshape(HEADS, HD),
         precision=lax.Precision.HIGHEST,
     )
     keyq = lax.all_gather(keyq_part, "dev", axis=0, tiled=True)
-    scale = jnp.sqrt(F32(HD))
-    if n % 8 or n // 8 < 2 or HEADS % n or D // n % 128 or tokens % (8 * (n // 8)) or tokens % CH:
-        grouped = lax.all_to_all(own_embed, "dev", split_axis=1, concat_axis=0, tiled=True)
-        logits = jnp.einsum(
-            "vtd,dh->vth", grouped.astype(F32), keyq, precision=lax.Precision.HIGHEST
-        ) / scale
-        return fallback_tail(grouped, softmax_slots(logits), value_t, out_w, n)
-    weights = jnp.concatenate([embed_w, var_embed[:, None, :]], axis=1)
-    weights = lax.all_to_all(weights, "dev", split_axis=2, concat_axis=0, tiled=True)
-    all_pixels = lax.all_gather(pixels, "dev", axis=0, tiled=True)
-    own_logits = jnp.einsum(
-        "vtd,dh->vth", own_embed.astype(F32), keyq, precision=lax.Precision.HIGHEST
-    ) / scale
-    logits = lax.all_gather(own_logits, "dev", axis=0, tiled=True)
-    attn = jnp.swapaxes(softmax_slots(logits), 0, 1)
-    patch = pixels.shape[2]
-    return fused_tail(
-        n, all_pixels, weights[:, :patch, :], weights[:, patch:, :].astype(F32), attn, value_t, out_w
-    )
+    logits = jnp.einsum(
+        "vtd,dh->vth", grouped.astype(jnp.float32), keyq, precision=lax.Precision.HIGHEST
+    ) / jnp.sqrt(jnp.float32(HD))
+    slot = lax.broadcasted_iota(jnp.int32, logits.shape, 0)
+    logits = jnp.where(slot < V, logits, -1e30)
+    row_max = jnp.max(logits, axis=0, keepdims=True)
+    weights = jnp.exp(logits - row_max)
+    attn = (weights / jnp.sum(weights, axis=0, keepdims=True)).astype(jnp.bfloat16)
+    pooled = jnp.einsum("vth,vtd->thd", attn, grouped, preferred_element_type=jnp.float32).astype(
+        jnp.bfloat16
+    )
+    own_tokens = pooled.shape[0]
+    if group_size >= HEADS:
+        spread = jnp.repeat(pooled, group_size // HEADS, axis=1)[:, :, None, :]
+    else:
+        spread = pooled.reshape(own_tokens, group_size, HEADS // group_size, D)
+    received = lax.all_to_all(spread, "dev", split_axis=1, concat_axis=0, tiled=True)
+    all_tokens = received.shape[0]
+    head_share = received.shape[2]
+    received = received.reshape(all_tokens, head_share, D)
+    columns = value_t.shape[0]
+    value_heads = jnp.einsum(
+        "thd,hcd->thc",
+        received,
+        value_t.reshape(head_share, columns // head_share, D),
+        preferred_element_type=jnp.float32,
+    )
+    value_heads = value_heads.reshape(all_tokens, columns).astype(jnp.bfloat16)
+    summed = lax.psum_scatter(
+        jnp.dot(value_heads, out_w, preferred_element_type=jnp.float32),
+        "dev",
+        scatter_dimension=0,
+        tiled=True,
+    )
+    return summed.astype(jnp.bfloat16)
+
+
+def body(pixels, embed_w, var_embed, key_w, query, value_t, out_w):
+    n = lax.axis_size("dev")
+    vs, tokens, patch = pixels.shape
+    dl = D // n
+    fits = (
+        n % 8 == 0 and n // 8 >= 2 and HEADS % n == 0 and dl == 2 * HD and patch % 16 == 0
+        and tokens % CH == 0 and tokens % (8 * (n // 8)) == 0 and vs * tokens <= dl
+    )
+    if not fits:
+        return plain_body(pixels, embed_w, var_embed, key_w, query, value_t, out_w)
+    turned = jnp.transpose(pixels, (2, 0, 1)).reshape(patch, vs * tokens)
+    turned = jnp.pad(turned, ((0, 0), (0, dl - vs * tokens)))
+    wp = jnp.concatenate([embed_w, jnp.tile(turned, (1, n))[None]], axis=0)
+    hi = lax.reduce_precision(query, 8, 7)
+    mid = lax.reduce_precision(query - hi, 8, 7)
+    low = query - hi - mid
+    parts = jnp.stack([hi, mid, low]).reshape(3, HEADS // 2, 1, 2, HD)
+    own = jnp.eye(2, dtype=F32)[None, None, :, :, None]
+    qtile = (parts * own).transpose(1, 0, 2, 3, 4).reshape(HEADS // 2, 6, 2 * HD)
+    qtile = jnp.pad(qtile, ((0, 0), (0, 10), (0, 0))).astype(BF16)
+    return fused_tail(n, pixels, wp, var_embed.astype(F32)[:, None, :], qtile, key_w, value_t, out_w)
 
 
 def solution(mesh):

time: 318 us -> 180 us (0.57)
  Pallas kernels: 92 us -> 171 us
  local copies, waits for them, and re-layouts: 65.7 us -> 4.8 us
  waiting for transfers between devices: 55.5 us -> 0 us
  blocking collectives: 51.5 us -> 0 us
  other arithmetic: 23.6 us -> 3.16 us
  between operations: 13.5 us -> 0.06 us
  matrix products: 10.9 us -> 0 us
  starting transfers between devices: 3.95 us -> 0 us
    pallas_call x1, Pallas kernels: 92 us -> 171 us  [fused_tail(): pl.pallas_call(functools.partial(tail_kernel, n), out_shape=jax.ShapeDtyp...]
    all_gather x2 -> x0, waiting for transfers between devices: 55.4 us -> none  [the longest x1 55.4 us: body(): keyq = lax.all_gather(keyq_part, 'dev', axis=0, tiled=True)]
    all_gather x1 -> x0, blocking collectives: 51.5 us -> none  [body(): all_pixels = lax.all_gather(pixels, 'dev', axis=0, tiled=True)]
    unnamed x14 -> x7, local copies, waits for them, and re-layouts: 36.9 us -> 2.12 us
    unnamed x1 -> x0, other arithmetic: 14.1 us -> none
    all_to_all x1 -> x0, local copies, waits for them, and re-layouts: 10.9 us -> none  [body(): lax.all_to_all(weights, 'dev', split_axis=2, concat_axis=0, tiled=True)]
    dot_general x3 -> x0, matrix products: 10.9 us -> none  [the longest x1 4.82 us: body(): jnp.einsum('vtd,dh->vth', own_embed.astype(F32), keyq, precision=lax.Prec...]
    broadcast_in_dim x1, local copies, waits for them, and re-layouts: 8.43 us -> 0.71 us  [body(): var_embed.astype(F32)[:, None, :]]
  transfers between devices with their start and end apart: 3 -> 0, of which waited for: 1 -> 0; matrix products, arithmetic and copies ran while one was open for 23% -> 0% of each run, Pallas kernels for 0% -> 0%
where the time goes in v2:
time: 180 us; the launch traced here: 179 us
  Pallas kernels  171 us (95%)
  local copies, waits for them, and re-layouts  4.8 us (3%)
  other arithmetic  3.16 us (2%)
    pallas_call x1, Pallas kernels, fused_tail(): pl.pallas_call(functools.partial(tail_kernel, n), out_shape=jax.ShapeDtyp...  171 us

profile of v2, /device:TPU:0, one launch (start us, length us, event | category | flops | bytes accessed | tf_op | source)
XLA Modules:
  0.0 179.1 jit_solution(11526913618613213405)
XLA Ops:
  0.0 0.0 copy-start.1
  0.0 0.0 copy-start
  0.0 0.8 fusion.1
  0.9 0.1 mul.27
  0.9 0.2 mul.28
  1.1 0.1 mul.29
  1.2 0.1 fusion
  1.3 0.7 pad.10.qtile
  2.0 0.7 copy.9
  2.7 0.1 reshape.27
  2.9 0.1 tile.9
  3.0 2.2 %pad_maximum_fusion.wp = bf16[4,16,8192]{2,1,0:T(8,128)(2,1)} fusion(bf16[1,16,8192]{2,1,0:T(8,128)(2,1)S(1)} %tile.9, bf16[3,16,8192]{2,1,0:T(8,128)(2,1)} %param.8), kind=kLoop, calls=%fused_computation | loop fusion | flops 524288 | bytes 2097152 | tf_op jit(solution)/shard_map/concatenate | solution.py:495
  5.2 0.0 copy-done
  5.2 0.7 reshape.28.var
  5.9 0.0 copy-done.1
  5.9 0.7 copy.11.pix
  6.6 171.0 %shard_map.73 = bf16[2,8192]{1,0:T(2,128)(2,1)} custom-call(bf16[3,64,16]{2,1,0:T(8,128)(2,1)} %copy.11.pix, bf16[4,16,8192]{2,1,0:T(8,128)(2,1)} %pad_maximum_fusion.wp, f32[3,1,8192]{2,1,0:T(1,128)} %reshape.28.var, bf16[32,16,256]{2,1,0:T(8,128)(2,1)} %pad.10.qtile, bf16[256,8192]{1,0:T(8,128)(2,1)} %key_hbm.1, bf16[256,8192]{1,0:T(8,128)(2,1)} %value_hbm.1, ...), custom_call_target="tpu_custom_call" | custom-call | tf_op jit(solution)/shard_map/pallas_call | solution.py:394
  177.7 1.4 copy.19
  (5 shorter events, 0.1 us)
Async XLA Ops:
  0.0 5.9 %copy-start.1 = (bf16[3,64,16]{1,2,0:T(8,128)(2,1)S(1)}, bf16[3,64,16]{1,2,0:T(8,128)(2,1)}, u32[]{:S(2)}) copy-start(bf16[3,64,16]{1,2,0:T(8,128)(2,1)} %param.7) | copy-start | bytes 18436
  0.0 5.2 %copy-start = (bf16[3,8192]{1,0:T(4,128)(2,1)S(1)}, bf16[3,8192]{1,0:T(4,128)(2,1)}, u32[]{:S(2)}) copy-start(bf16[3,8192]{1,0:T(4,128)(2,1)} %param.9) | copy-start | bytes 147460

commit v3 on v2

--- a/solution.py
+++ b/solution.py
@@ -63,16 +63,18 @@
         c2 = go(k + 6, buf.at[pl.ds(qy * nz, nz)], other)
         return fy, fx, c0, c1, c2
 
-    def finish(fy, fx, c0, c1, c2):
+    def diagonal(fy, fx, c0, c1, c2):
         fy.wait_recv()
         fx.wait_recv()
-        c3 = go(nz + 6, buf.at[pl.ds(qd * nz, nz)], other)
-        for cp in (c0, c1, c2, c3):
+        return c0, c1, c2, go(nz + 6, buf.at[pl.ds(qd * nz, nz)], other)
+
+    def finish(copies):
+        for cp in copies:
             cp.wait_recv()
         for cp in started:
             cp.wait_send()
 
-    return along_z, rest, finish
+    return along_z, rest, diagonal, finish
 
 
 def tail_kernel(
@@ -125,8 +127,8 @@
             preferred_element_type=F32,
         )
         kq[mine, 2 * kt:2 * kt + 2, :] = r[0:2] + r[2:4] + r[4:6]
-    kq_z, kq_rest, kq_finish = gather_steps(kq, gsend, grecv, me, nz)
-    lg_z, lg_rest, lg_finish = gather_steps(lg, hsend, hrecv, me, nz)
+    kq_z, kq_rest, kq_diag, kq_finish = gather_steps(kq, gsend, grecv, me, nz)
+    lg_z, lg_rest, lg_diag, lg_finish = gather_steps(lg, hsend, hrecv, me, nz)
     kq_z()
 
     def own_one(s, carry):
@@ -141,12 +143,14 @@
     lax.fori_loop(n // 2, n, own_one, 0)
     wall[me] = wp[:, :, cols_of(me)]
     vall[me] = var[:, :, cols_of(me)]
-    kq_finish(*state)
+    state = kq_diag(*state)
     lax.fori_loop(early, n // 2, w_send, 0)
     lax.fori_loop(n // 2 + 1, n, w_send, 0)
 
-    def logit_one(s, acc):
-        a = kq[slot_of(s, nz)]
+    def logit_one(slot, acc):
+        place = slot // nz
+        s = slot % nz * 8 + (place // 2) % 2 * 4 + place % 2 * 2 + place // 4
+        a = kq[slot]
         hi = a.astype(BF16)
         rest = a - hi.astype(F32)
         mid = rest.astype(BF16)
@@ -156,7 +160,11 @@
             oemb[:, cols_of(s)], b, (((1,), (1,)), ((), ())), preferred_element_type=F32
         )
 
-    acc = lax.fori_loop(0, n, logit_one, jnp.zeros((vs * tokens, 3 * HEADS), F32))
+    half_n = 4 * nz
+    acc = jnp.zeros((vs * tokens, 3 * HEADS), F32)
+    acc = lax.fori_loop(0, half_n, lambda i, a: logit_one(core * half_n + i, a), acc)
+    kq_finish(state)
+    acc = lax.fori_loop(0, half_n, lambda i, a: logit_one((1 - core) * half_n + i, a), acc)
     logit = (acc[:, :HEADS] + acc[:, HEADS:2 * HEADS] + acc[:, 2 * HEADS:]) / jnp.sqrt(F32(HD))
     for v in range(vs):
         pair = jnp.concatenate(
@@ -176,35 +184,42 @@
                 embf[k, pl.ds(at + v, tokens, stride=slots), :] = e[:, k * 128:(k + 1) * 128]
 
     def arrive_w(i, carry):
-        s = (me + i) % n
+        s = (me + n + n // 2 - i) % n
         w_copy(s, s).wait_recv()
         v_copy(s, s).wait_recv()
         embed_one(s)
         return carry
 
     embed_one(me)
+    lax.fori_loop(0, early, arrive_w, 0)
     state = lg_rest()
-    lax.fori_loop(1, n, arrive_w, 0)
-    lg_finish(*state)
-    for g in range(ht // 8):
-        def at_v(v, g=g):
-            return lg[v // vs, pl.ds(pl.multiple_of(v % vs * ht + g * 8, 8), 8), :]
-
-        top = lax.fori_loop(1, slots, lambda v, m: jnp.maximum(m, at_v(v)), at_v(0), unroll=4)
-
-        def exp_one(v, total, g=g, at_v=at_v, top=top):
-            e = jnp.exp(at_v(v) - top)
-            prob[pl.ds(pl.multiple_of(v * ht + g * 8, 8), 8), :] = e
-            return total + e
-
-        total = lax.fori_loop(0, slots, exp_one, jnp.zeros((8, 128), F32), unroll=4)
-
-        def div_one(v, carry, g=g, total=total):
-            rows = pl.ds(pl.multiple_of(v * ht + g * 8, 8), 8)
+    lax.fori_loop(early, n // 2, arrive_w, 0)
+    state = lg_diag(*state)
+    lax.fori_loop(n // 2 + 1, n, arrive_w, 0)
+    lg_finish(state)
+    def top_one(k, top):
+        for v in range(vs):
+            top = jnp.maximum(top, lg[k, v * ht:(v + 1) * ht, :])
+        return top
+
+    top = lax.fori_loop(0, n, top_one, lg[0, :ht, :], unroll=4)
+
+    def exp_one(k, total):
+        for v in range(vs):
+            e = jnp.exp(lg[k, v * ht:(v + 1) * ht, :] - top)
+            prob[pl.ds(pl.multiple_of((k * vs + v) * ht, 8), ht), :] = e
+            total = total + e
+        return total
+
+    total = lax.fori_loop(0, n, exp_one, jnp.zeros((ht, 2 * HEADS), F32), unroll=2)
+
+    def div_one(k, carry):
+        for v in range(vs):
+            rows = pl.ds(pl.multiple_of((k * vs + v) * ht, 8), ht)
             prob[rows, :] = prob[rows, :] / total
-            return carry
-
-        lax.fori_loop(0, slots, div_one, 0, unroll=4)
+        return carry
+
+    lax.fori_loop(0, n, div_one, 0, unroll=2)
 
     def exchange(c, partner, slot):
         return pltpu.make_async_remote_copy(

time: 180 us -> 163 us (0.906)
  Pallas kernels: 171 us -> 154 us
    pallas_call x1, Pallas kernels: 171 us -> 154 us  [fused_tail(): pl.pallas_call(functools.partial(tail_kernel, n), out_shape=jax.ShapeDtyp...]
where the time goes in v3:
time: 163 us; the launch traced here: 162 us
  Pallas kernels  154 us (94%)
  local copies, waits for them, and re-layouts  4.8 us (3%)
  other arithmetic  3.16 us (2%)
    pallas_call x1, Pallas kernels, fused_tail(): pl.pallas_call(functools.partial(tail_kernel, n), out_shape=jax.ShapeDtyp...  154 us

profile of v3, /device:TPU:0, one launch (start us, length us, event | category | flops | bytes accessed | tf_op | source)
XLA Modules:
  0.0 162.2 jit_solution(4022408833815437541)
XLA Ops:
  0.0 0.0 copy-start.1
  0.0 0.0 copy-start
  0.0 0.8 fusion.1
  0.9 0.1 mul.27
  0.9 0.2 mul.28
  1.1 0.1 mul.29
  1.2 0.1 fusion
  1.3 0.7 pad.10.qtile
  2.0 0.7 copy.9
  2.7 0.1 reshape.27
  2.9 0.1 tile.9
  3.0 2.2 %pad_maximum_fusion.wp = bf16[4,16,8192]{2,1,0:T(8,128)(2,1)} fusion(bf16[1,16,8192]{2,1,0:T(8,128)(2,1)S(1)} %tile.9, bf16[3,16,8192]{2,1,0:T(8,128)(2,1)} %param.8), kind=kLoop, calls=%fused_computation | loop fusion | flops 524288 | bytes 2097152 | tf_op jit(solution)/shard_map/concatenate | solution.py:510
  5.2 0.0 copy-done
  5.2 0.7 reshape.28.var
  5.9 0.0 copy-done.1
  5.9 0.7 copy.11.pix
  6.6 154.2 %shard_map.73 = bf16[2,8192]{1,0:T(2,128)(2,1)} custom-call(bf16[3,64,16]{2,1,0:T(8,128)(2,1)} %copy.11.pix, bf16[4,16,8192]{2,1,0:T(8,128)(2,1)} %pad_maximum_fusion.wp, f32[3,1,8192]{2,1,0:T(1,128)} %reshape.28.var, bf16[32,16,256]{2,1,0:T(8,128)(2,1)} %pad.10.qtile, bf16[256,8192]{1,0:T(8,128)(2,1)} %key_hbm.1, bf16[256,8192]{1,0:T(8,128)(2,1)} %value_hbm.1, ...), custom_call_target="tpu_custom_call" | custom-call | tf_op jit(solution)/shard_map/pallas_call | solution.py:409
  160.8 1.4 copy.19
  (5 shorter events, 0.1 us)
Async XLA Ops:
  0.0 5.9 %copy-start.1 = (bf16[3,64,16]{1,2,0:T(8,128)(2,1)S(1)}, bf16[3,64,16]{1,2,0:T(8,128)(2,1)}, u32[]{:S(2)}) copy-start(bf16[3,64,16]{1,2,0:T(8,128)(2,1)} %param.7) | copy-start | bytes 18436
  0.0 5.2 %copy-start = (bf16[3,8192]{1,0:T(4,128)(2,1)S(1)}, bf16[3,8192]{1,0:T(4,128)(2,1)}, u32[]{:S(2)}) copy-start(bf16[3,8192]{1,0:T(4,128)(2,1)} %param.9) | copy-start | bytes 147460
